TPU v7x, 32 devices: a whole 2x2x4 slice. The times are simulated.
32 devices in a mesh: dp: 2 (over core), gx: 4 (over y, x), gy: 4 (over z).
Axes of the slice: x: 2, y: 2, z: 4, core: 2. Of those that a mesh axis runs over, the one named last changes fastest.
Arguments:
- volume: bfloat16 [2, 4, 8, 32, 128], P('dp', None, 'gx', 'gy'), may hold values from -6 to 6
- targets: float32 [2, 4], P('dp'), may hold values from -4 to 4
- conv1_w: bfloat16 [27, 128], replicated, may hold values from -0.625 to 0.625
- conv1_b: float32 [32], replicated, may hold values from -3 to 3
- conv2_w: bfloat16 [27, 2048], replicated, may hold values from -0.21875 to 0.21875
- conv2_b: float32 [64], replicated, may hold values from -3 to 3
- head_w: float32 [64, 4], replicated, may hold values from -2 to 2
- head_b: float32 [4], replicated, may hold values from -4 to 4
- dir1: float32 [27, 128], replicated, may hold values from -6 to 6
- dir2: float32 [27, 2048], replicated, may hold values from -1.2 to 1.2
- dir_head: float32 [64, 4], replicated, may hold values from -6 to 6
Outputs:
- next1: float32 [27, 128], replicated
- next2: float32 [27, 2048], replicated
- next_head: float32 [64, 4], replicated
- rayleigh: float32 [], replicated
- curvature_field: float32 [2, 32, 8, 32, 128], P('dp', None, 'gx', 'gy')
All inputs are finite; a program needn't handle non-finite values.
Results may differ from a plain program's by a relative error of at most 0.0051.
Values may be sent and summed in bfloat16 or wider, within the bound.
A program may use at most 128 MiB of HBM per device.

v0:
```python
import jax
import jax.numpy as jnp
from jax import lax
from jax.sharding import PartitionSpec as P

C0 = 4
C1 = 32
C2 = 64


def extended(cells, sides, width):
    for axis, dim in sides:
        count = lax.axis_size(axis)
        ends = count - 1
        head = lax.slice_in_dim(cells, 0, width, axis=dim)
        tail = lax.slice_in_dim(cells, cells.shape[dim] - width, cells.shape[dim], axis=dim)
        cells = jnp.concatenate(
            [
                lax.ppermute(tail, axis, [(i, (i + 1) % count) for i in range(ends)]),
                cells,
                lax.ppermute(head, axis, [((i + 1) % count, i) for i in range(ends)]),
            ],
            axis=dim,
        )
    return cells


def silu_parts(z):
    s = jax.nn.sigmoid(z)
    return (z * s, s * (1.0 + z * (1.0 - s)), s * (1.0 - s) * (2.0 + z * (1.0 - 2.0 * s)))


def as_kernel(flat, outer, inner):
    return flat.reshape(3, 3, 3, outer, inner).transpose(3, 4, 0, 1, 2)


def pad_depth(a):
    return jnp.pad(a, ((0, 0), (0, 0), (0, 0), (0, 0), (1, 1)))


def convolve(padded, kernel):
    return lax.conv_general_dilated(
        pad_depth(padded),
        kernel,
        (1, 1, 1),
        "VALID",
        dimension_numbers=("NCDHW", "OIDHW", "NCDHW"),
        preferred_element_type=jnp.float32,
    )


def flipped(kernel):
    return jnp.flip(kernel, (2, 3, 4)).transpose(1, 0, 2, 3, 4)


def correlate(padded, grads):
    wide = pad_depth(padded)
    sx, sy, sz = (grads.shape[2], grads.shape[3], grads.shape[4])
    pieces = []
    for a in range(3):
        for b in range(3):
            for c in range(3):
                window = wide[:, :, a : a + sx, b : b + sy, c : c + sz]
                pieces.append(
                    jnp.einsum("bixyz,boxyz->oi", window, grads, preferred_element_type=jnp.float32)
                )
    stacked = jnp.stack(pieces, axis=0)
    return stacked.reshape(27, grads.shape[1] * padded.shape[1])


def spread(vector):
    return vector[:, :, None, None, None]


def per_device(
    volume, targets, conv1_w, conv1_b, conv2_w, conv2_b, head_w, head_b, dir1, dir2, dir_head
):
    high = lax.Precision.HIGHEST
    weight1 = as_kernel(conv1_w, C1, C0)
    weight2 = as_kernel(conv2_w, C2, C1)
    kern1 = as_kernel(dir1.astype(jnp.bfloat16), C1, C0)
    kern2 = as_kernel(dir2.astype(jnp.bfloat16), C2, C1)
    depth, height = (volume.shape[2], volume.shape[3])
    padded_in = extended(volume, (("gx", 2), ("gy", 3)), 1)
    z1 = convolve(padded_in, weight1) + conv1_b[None, :, None, None, None]
    t1 = convolve(padded_in, kern1)
    act1, slope1, bend1 = silu_parts(z1)
    a1 = act1.astype(jnp.bfloat16)
    ta1 = (slope1 * t1).astype(jnp.bfloat16)
    pa1 = extended(a1, (("gx", 2), ("gy", 3)), 1)
    pta1 = extended(ta1, (("gx", 2), ("gy", 3)), 1)
    z2 = convolve(pa1, weight2) + conv2_b[None, :, None, None, None]
    t2 = convolve(pta1, weight2) + convolve(pa1, kern2)
    act2, slope2, bend2 = silu_parts(z2)
    width = z2.shape[4]
    cells = depth * lax.axis_size("gx") * height * lax.axis_size("gy") * width
    sums = lax.psum(
        (jnp.sum(act2, axis=(2, 3, 4)), jnp.sum(slope2 * t2, axis=(2, 3, 4))), ("gx", "gy")
    )
    pooled = sums[0] / cells
    tpooled = sums[1] / cells
    batch = volume.shape[0] * lax.axis_size("dp")
    outputs = jnp.dot(pooled, head_w, precision=high) + head_b
    toutputs = jnp.dot(tpooled, head_w, precision=high) + jnp.dot(pooled, dir_head, precision=high)
    dy = (outputs - targets) / batch
    tdy = toutputs / batch
    leader = ((lax.axis_index("gx") == 0) & (lax.axis_index("gy") == 0)).astype(jnp.float32)
    hd = leader * (jnp.dot(tpooled.T, dy, precision=high) + jnp.dot(pooled.T, tdy, precision=high))
    dpool = jnp.dot(dy, head_w.T, precision=high) / cells
    tdpool = (
        jnp.dot(tdy, head_w.T, precision=high) + jnp.dot(dy, dir_head.T, precision=high)
    ) / cells
    g2 = (slope2 * spread(dpool)).astype(jnp.bfloat16)
    tg2 = (bend2 * t2 * spread(dpool) + slope2 * spread(tdpool)).astype(jnp.bfloat16)
    back_w = flipped(weight2)
    back_k = flipped(kern2)
    joined = extended(jnp.stack((g2, tg2)), (("gx", 3), ("gy", 4)), 1)
    pg2, ptg2 = (joined[0], joined[1])
    da1 = convolve(pg2, back_w)
    tda1 = convolve(ptg2, back_w) + convolve(pg2, back_k)
    tg1 = (bend1 * t1 * da1 + slope1 * tda1).astype(jnp.bfloat16)
    h1 = correlate(padded_in, tg1)
    h2 = correlate(pa1, tg2) + correlate(pta1, g2)
    h1, h2, hd = lax.psum((h1, h2, hd), ("dp", "gx", "gy"))
    field = tda1 * cells
    quad = jnp.sum(dir1 * h1) + jnp.sum(dir2 * h2) + jnp.sum(dir_head * hd)
    length = jnp.sum(dir1 * dir1) + jnp.sum(dir2 * dir2) + jnp.sum(dir_head * dir_head)
    nrm = jnp.sqrt(jnp.sum(h1 * h1) + jnp.sum(h2 * h2) + jnp.sum(hd * hd) + 1e-06)
    return (h1 / nrm, h2 / nrm, hd / nrm, quad / length, field)


def solution(mesh):
    return jax.shard_map(
        per_device,
        mesh=mesh,
        in_specs=(
            P("dp", None, "gx", "gy", None),
            P("dp", None),
            P(),
            P(),
            P(),
            P(),
            P(),
            P(),
            P(),
            P(),
            P(),
        ),
        out_specs=(P(), P(), P(), P(), P("dp", None, "gx", "gy", None)),
        check_vma=False,
    )
```

profile of v0, /device:TPU:0, one launch (start us, length us, event | category | flops | bytes accessed | tf_op | source)
XLA Modules:
  0.0 376.5 jit_solution(5744117732220031743)
XLA Ops:
  8.0 4.9 %collective-permute-start = (bf16[1,4,1,8,128]{4,1,3,2,0:T(4,128)(2,1)S(1)}, bf16[1,4,1,8,128]{4,1,3,2,0:T(4,128)(2,1)S(1)}, u32[]{:S(2)}, u32[]{:S(2)}) collective-permute-start(bf16[1,4,1,8,128]{4,1,3,2,0:T(4,128)(2,1)S(1)} %get-tuple-element.60), channel_id=1, source_target_pairs={{0,4},{4,8},{8,12},{1,5},{5,9},{9,13},{2,6},{6,10},{10,14},{3,7},{... | collective-permute-start | bytes 24584 | tf_op jit(solution)/shard_map/ppermute | solution.py:19
  15.0 3.5 collective-permute-done.1
  19.8 4.5 %collective-permute-start.2 = (bf16[1,4,4,1,128]{4,1,3,2,0:T(4,128)(2,1)S(1)}, bf16[1,4,4,1,128]{4,1,3,2,0:T(4,128)(2,1)S(1)}, u32[]{:S(2)}, u32[]{:S(2)}) collective-permute-start(bf16[1,4,4,1,128]{4,1,3,2,0:T(4,128)(2,1)S(1)} %get-tuple-element.57), channel_id=1, source_target_pairs={{0,1},{1,2},{2,3},{4,5},{5,6},{6,7},{8,9},{9,10},{10,11},{12,13},{... | collective-permute-start | bytes 12296 | tf_op jit(solution)/shard_map/ppermute | solution.py:19
  24.3 2.0 reshape.567
  31.9 6.4 %fusion.38 = f32[2,8,8,17,32]{4,2,3,1,0:T(8,128)S(1)} fusion(bf16[3,3,3,32,4]{4,3,2,1,0:T(8,128)(2,1)S(1)} %reshape.565, f32[32]{0:T(128)S(1)} %copy-done.53, pred[8,17]{0,1:T(8,128)(4,1)S(1)} %copy-done.57, bf16[4,4,10,1,7,2]{4,0,5,2,1,3:T(4,128)(2,1)S(1)} %slice.473, bf16[4,4,10,1,8,17]{4,0,5,2,1,3:T(4,128)(2,1)S(1)} %copy.299), kind=kOutput, calls=%fused_computation.77 | convolution fusion | flops 15325696 | bytes 333704 | tf_op jit(solution)/shard_map/conv_general_dilated | solution.py:42
  38.3 7.7 %multiply_convert_fusion.1 = (bf16[2,8,8,17,32]{4,2,3,1,0:T(8,128)(2,1)S(1)}, bf16[2,8,8,17,32]{4,2,3,1,0:T(8,128)(2,1)S(1)}, f32[2,8,8,17,32]{4,2,3,1,0:T(8,128)}) fusion(f32[2,8,8,17,32]{4,2,3,1,0:T(8,128)S(1)} %fusion.38, bf16[3,3,3,32,4]{4,3,2,1,0:T(8,128)(2,1)S(1)} %reshape.566, bf16[4,4,10,1,7,2]{4,0,5,2,1,3:T(4,128)(2,1)S(1)} %slice.473, ...), kind=kOutput, calls=%fused_computation.95 | convolution fusion | flops 16022016 | bytes 890632 | tf_op jit(solution)/shard_map/conv_general_dilated | solution.py:42
  48.4 4.9 %collective-permute-start.4 = (bf16[1,32,1,8,128]{4,1,3,2,0:T(8,128)(2,1)S(1)}, bf16[1,32,1,8,128]{4,1,3,2,0:T(8,128)(2,1)S(1)}, u32[]{:S(2)}, u32[]{:S(2)}) collective-permute-start(bf16[1,32,1,8,128]{4,1,3,2,0:T(8,128)(2,1)S(1)} %bitcast.755), channel_id=1, source_target_pairs={{0,4},{4,8},{8,12},{1,5},{5,9},{9,13},{2,6},{6,10},{10,14},{3,7},{... | collective-permute-start | bytes 196616 | tf_op jit(solution)/shard_map/ppermute | solution.py:19
  55.6 5.4 %collective-permute-start.8 = (bf16[1,32,1,8,128]{4,1,3,2,0:T(8,128)(2,1)S(1)}, bf16[1,32,1,8,128]{4,1,3,2,0:T(8,128)(2,1)S(1)}, u32[]{:S(2)}, u32[]{:S(2)}) collective-permute-start(bf16[1,32,1,8,128]{4,1,3,2,0:T(8,128)(2,1)S(1)} %bitcast.756), channel_id=1, source_target_pairs={{0,4},{4,8},{8,12},{1,5},{5,9},{9,13},{2,6},{6,10},{10,14},{3,7},{... | collective-permute-start | bytes 196616 | tf_op jit(solution)/shard_map/ppermute | solution.py:19
  62.5 4.5 %collective-permute-start.6 = (bf16[1,32,4,1,128]{4,1,3,2,0:T(8,128)(2,1)S(1)}, bf16[1,32,4,1,128]{4,1,3,2,0:T(8,128)(2,1)S(1)}, u32[]{:S(2)}, u32[]{:S(2)}) collective-permute-start(bf16[1,32,4,1,128]{4,1,3,2,0:T(8,128)(2,1)S(1)} %get-tuple-element.55), channel_id=1, source_target_pairs={{0,1},{1,2},{2,3},{4,5},{5,6},{6,7},{8,9},{9,10},{10,11},{12,13},{... | collective-permute-start | bytes 98312 | tf_op jit(solution)/shard_map/ppermute | solution.py:19
  69.0 4.5 %collective-permute-start.10 = (bf16[1,32,4,1,128]{4,1,3,2,0:T(8,128)(2,1)}, bf16[1,32,4,1,128]{4,1,3,2,0:T(8,128)(2,1)S(1)}, u32[]{:S(2)}, u32[]{:S(2)}) collective-permute-start(bf16[1,32,4,1,128]{4,1,3,2,0:T(8,128)(2,1)} %get-tuple-element.53), channel_id=1, source_target_pairs={{0,1},{1,2},{2,3},{4,5},{5,6},{6,7},{8,9},{9,10},{10,11},{12,13},{... | collective-permute-start | bytes 98312 | tf_op jit(solution)/shard_map/ppermute | solution.py:19
  78.7 1.9 convolution_select_fusion.2
  80.7 1.9 fusion.37
  82.7 2.4 select_reduce_fusion
  85.1 39.3 %all-reduce.4 = (f32[1,64]{1,0:T(1,128)S(1)}, f32[1,64]{1,0:T(1,128)S(1)}) all-reduce(f32[1,64]{1,0:T(1,128)S(1)} %bitcast.760, f32[1,64]{1,0:T(1,128)S(1)} %bitcast.759), channel_id=1, replica_groups=mesh['dp'=2,'gx'=4,'gy'=4] {'gx','gy'}, use_global_device_ids=true, to_apply=%region_1.2 | all-reduce | flops 128 | bytes 1024 | tf_op jit(solution)/shard_map/psum | solution.py:97
  126.2 2.1 multiply_convert_fusion
  151.0 4.6 %collective-permute-start.12 = (bf16[2,1,64,1,8,128]{5,2,4,3,1,0:T(8,128)(2,1)S(1)}, bf16[2,1,64,1,8,128]{5,2,4,3,1,0:T(8,128)(2,1)S(1)}, u32[]{:S(2)}, u32[]{:S(2)}) collective-permute-start(bf16[2,1,64,1,8,128]{5,2,4,3,1,0:T(8,128)(2,1)S(1)} %get-tuple-element.47), channel_id=1, source_target_pairs={{0,4},{4,8},{8,12},{1,5},{5,9},{9,13},{2,6},{6,10},{10,14},{3,7},{... | collective-permute-start | bytes 786440 | tf_op jit(solution)/shard_map/ppermute | solution.py:19
  165.2 4.6 %collective-permute-start.14 = (bf16[2,1,64,4,1,128]{5,2,4,3,1,0:T(8,128)(2,1)S(1)}, bf16[2,1,64,4,1,128]{5,2,4,3,1,0:T(8,128)(2,1)S(1)}, u32[]{:S(2)}, u32[]{:S(2)}) collective-permute-start(bf16[2,1,64,4,1,128]{5,2,4,3,1,0:T(8,128)(2,1)S(1)} %get-tuple-element.41), channel_id=1, source_target_pairs={{0,1},{1,2},{2,3},{4,5},{5,6},{6,7},{8,9},{9,10},{10,11},{12,13},{... | collective-permute-start | bytes 393224 | tf_op jit(solution)/shard_map/ppermute | solution.py:19
  169.7 121.5 %all-reduce.7.cloned.1.call-done = f32[27,2048]{1,0:T(8,128)} async-done(((f32[27,2048]{1,0:T(8,128)}), f32[27,2048]{1,0:T(8,128)}) %all-reduce.7.cloned.1.call-update) | async-done | bytes 221200 | tf_op jit(solution)/shard_map/psum | solution.py:124
  291.3 1.7 multiply_reduce_fusion
  296.7 3.3 convolution_select_fusion
  300.0 1.8 copy.592
  303.9 2.4 broadcast_multiply_fusion
  306.3 2.7 fusion.39
  318.4 39.5 %all-reduce.3 = (f32[27,128]{1,0:T(8,128)S(1)}, f32[64,4]{0,1:T(4,128)S(1)}) all-reduce(f32[27,128]{1,0:T(8,128)S(1)} %stack.291, f32[64,4]{0,1:T(4,128)S(1)} %add_multiply_fusion), channel_id=1, replica_groups=mesh['dp'=2,'gx'=4,'gy'=4] {'dp','gx','gy'}, use_global_device_ids=true, to_apply=%region_4.5 | all-reduce | flops 3712 | bytes 29696 | tf_op jit(solution)/shard_map/psum | solution.py:124
  (408 shorter events, 75.2 us)
Async XLA Ops:
  7.2 117.2 %copy-start = (f32[64,4]{0,1:T(4,128)S(1)}, f32[64,4]{0,1:T(4,128)}, u32[]{:S(2)}) copy-start(f32[64,4]{0,1:T(4,128)} %param.17) | copy-start | bytes 3076
  7.2 284.1 %all-reduce.7.cloned.1.call-start = ((), (), s32[]{:S(2)}) async-start(), calls=%async_computation | async-start | bytes 524288 | tf_op jit(solution)/shard_map/psum | solution.py:124
  8.0 6.2 %collective-permute-start = (bf16[1,4,1,8,128]{4,1,3,2,0:T(4,128)(2,1)S(1)}, bf16[1,4,1,8,128]{4,1,3,2,0:T(4,128)(2,1)S(1)}, u32[]{:S(2)}, u32[]{:S(2)}) collective-permute-start(bf16[1,4,1,8,128]{4,1,3,2,0:T(4,128)(2,1)S(1)} %get-tuple-element.60), channel_id=1, source_target_pairs={{0,4},{4,8},{8,12},{1,5},{5,9},{9,13},{2,6},{6,10},{10,14},{3,7},{... | collective-permute-start | bytes 24584 | tf_op jit(solution)/shard_map/ppermute | solution.py:19
  12.9 5.5 %collective-permute-start.1 = (bf16[1,4,1,8,128]{4,1,3,2,0:T(4,128)(2,1)S(1)}, bf16[1,4,1,8,128]{4,1,3,2,0:T(4,128)(2,1)S(1)}, u32[]{:S(2)}, u32[]{:S(2)}) collective-permute-start(bf16[1,4,1,8,128]{4,1,3,2,0:T(4,128)(2,1)S(1)} %get-tuple-element.59), channel_id=1, source_target_pairs={{4,0},{8,4},{12,8},{5,1},{9,5},{13,9},{6,2},{10,6},{14,10},{7,3},{... | collective-permute-start | bytes 24584 | tf_op jit(solution)/shard_map/ppermute | solution.py:21
  18.4 42.6 %copy-start.28 = (bf16[1,4,4,8,128]{4,1,3,2,0:T(4,128)(2,1)}, bf16[1,4,4,8,128]{4,1,3,2,0:T(4,128)(2,1)S(1)}, u32[]{:S(2)}) copy-start(bf16[1,4,4,8,128]{4,1,3,2,0:T(4,128)(2,1)S(1)} %constant_dynamic-update-slice_fusion) | copy-start | bytes 98308
  18.5 11.4 %collective-permute-start.3 = (bf16[1,4,4,1,128]{4,1,3,2,0:T(4,128)(2,1)S(1)}, bf16[1,4,4,1,128]{4,1,3,2,0:T(4,128)(2,1)S(1)}, u32[]{:S(2)}, u32[]{:S(2)}) collective-permute-start(bf16[1,4,4,1,128]{4,1,3,2,0:T(4,128)(2,1)S(1)} %get-tuple-element.58), channel_id=1, source_target_pairs={{1,0},{2,1},{3,2},{5,4},{6,5},{7,6},{9,8},{10,9},{11,10},{13,12},{... | collective-permute-start | bytes 12296 | tf_op jit(solution)/shard_map/ppermute | solution.py:21
  19.8 10.1 %collective-permute-start.2 = (bf16[1,4,4,1,128]{4,1,3,2,0:T(4,128)(2,1)S(1)}, bf16[1,4,4,1,128]{4,1,3,2,0:T(4,128)(2,1)S(1)}, u32[]{:S(2)}, u32[]{:S(2)}) collective-permute-start(bf16[1,4,4,1,128]{4,1,3,2,0:T(4,128)(2,1)S(1)} %get-tuple-element.57), channel_id=1, source_target_pairs={{0,1},{1,2},{2,3},{4,5},{5,6},{6,7},{8,9},{9,10},{10,11},{12,13},{... | collective-permute-start | bytes 12296 | tf_op jit(solution)/shard_map/ppermute | solution.py:19
  46.5 14.6 %collective-permute-start.5 = (bf16[1,32,1,8,128]{4,1,3,2,0:T(8,128)(2,1)S(1)}, bf16[1,32,1,8,128]{4,1,3,2,0:T(8,128)(2,1)S(1)}, u32[]{:S(2)}, u32[]{:S(2)}) collective-permute-start(bf16[1,32,1,8,128]{4,1,3,2,0:T(8,128)(2,1)S(1)} %bitcast.753), channel_id=1, source_target_pairs={{4,0},{8,4},{12,8},{5,1},{9,5},{13,9},{6,2},{10,6},{14,10},{7,3},{... | collective-permute-start | bytes 196616 | tf_op jit(solution)/shard_map/ppermute | solution.py:21
  48.4 12.7 %collective-permute-start.4 = (bf16[1,32,1,8,128]{4,1,3,2,0:T(8,128)(2,1)S(1)}, bf16[1,32,1,8,128]{4,1,3,2,0:T(8,128)(2,1)S(1)}, u32[]{:S(2)}, u32[]{:S(2)}) collective-permute-start(bf16[1,32,1,8,128]{4,1,3,2,0:T(8,128)(2,1)S(1)} %bitcast.755), channel_id=1, source_target_pairs={{0,4},{4,8},{8,12},{1,5},{5,9},{9,13},{2,6},{6,10},{10,14},{3,7},{... | collective-permute-start | bytes 196616 | tf_op jit(solution)/shard_map/ppermute | solution.py:19
  53.6 13.4 %collective-permute-start.9 = (bf16[1,32,1,8,128]{4,1,3,2,0:T(8,128)(2,1)S(1)}, bf16[1,32,1,8,128]{4,1,3,2,0:T(8,128)(2,1)S(1)}, u32[]{:S(2)}, u32[]{:S(2)}) collective-permute-start(bf16[1,32,1,8,128]{4,1,3,2,0:T(8,128)(2,1)S(1)} %bitcast.754), channel_id=1, source_target_pairs={{4,0},{8,4},{12,8},{5,1},{9,5},{13,9},{6,2},{10,6},{14,10},{7,3},{... | collective-permute-start | bytes 196616 | tf_op jit(solution)/shard_map/ppermute | solution.py:21
  55.6 11.5 %collective-permute-start.8 = (bf16[1,32,1,8,128]{4,1,3,2,0:T(8,128)(2,1)S(1)}, bf16[1,32,1,8,128]{4,1,3,2,0:T(8,128)(2,1)S(1)}, u32[]{:S(2)}, u32[]{:S(2)}) collective-permute-start(bf16[1,32,1,8,128]{4,1,3,2,0:T(8,128)(2,1)S(1)} %bitcast.756), channel_id=1, source_target_pairs={{0,4},{4,8},{8,12},{1,5},{5,9},{9,13},{2,6},{6,10},{10,14},{3,7},{... | collective-permute-start | bytes 196616 | tf_op jit(solution)/shard_map/ppermute | solution.py:19
  61.2 12.4 %collective-permute-start.7 = (bf16[1,32,4,1,128]{4,1,3,2,0:T(8,128)(2,1)S(1)}, bf16[1,32,4,1,128]{4,1,3,2,0:T(8,128)(2,1)S(1)}, u32[]{:S(2)}, u32[]{:S(2)}) collective-permute-start(bf16[1,32,4,1,128]{4,1,3,2,0:T(8,128)(2,1)S(1)} %get-tuple-element.56), channel_id=1, source_target_pairs={{1,0},{2,1},{3,2},{5,4},{6,5},{7,6},{9,8},{10,9},{11,10},{13,12},{... | collective-permute-start | bytes 98312 | tf_op jit(solution)/shard_map/ppermute | solution.py:21
  62.5 11.1 %collective-permute-start.6 = (bf16[1,32,4,1,128]{4,1,3,2,0:T(8,128)(2,1)S(1)}, bf16[1,32,4,1,128]{4,1,3,2,0:T(8,128)(2,1)S(1)}, u32[]{:S(2)}, u32[]{:S(2)}) collective-permute-start(bf16[1,32,4,1,128]{4,1,3,2,0:T(8,128)(2,1)S(1)} %get-tuple-element.55), channel_id=1, source_target_pairs={{0,1},{1,2},{2,3},{4,5},{5,6},{6,7},{8,9},{9,10},{10,11},{12,13},{... | collective-permute-start | bytes 98312 | tf_op jit(solution)/shard_map/ppermute | solution.py:19
  67.7 8.4 %collective-permute-start.11 = (bf16[1,32,4,1,128]{4,1,3,2,0:T(8,128)(2,1)}, bf16[1,32,4,1,128]{4,1,3,2,0:T(8,128)(2,1)S(1)}, u32[]{:S(2)}, u32[]{:S(2)}) collective-permute-start(bf16[1,32,4,1,128]{4,1,3,2,0:T(8,128)(2,1)} %get-tuple-element.54), channel_id=1, source_target_pairs={{1,0},{2,1},{3,2},{5,4},{6,5},{7,6},{9,8},{10,9},{11,10},{13,12},{... | collective-permute-start | bytes 98312 | tf_op jit(solution)/shard_map/ppermute | solution.py:21
  69.0 7.1 %collective-permute-start.10 = (bf16[1,32,4,1,128]{4,1,3,2,0:T(8,128)(2,1)}, bf16[1,32,4,1,128]{4,1,3,2,0:T(8,128)(2,1)S(1)}, u32[]{:S(2)}, u32[]{:S(2)}) collective-permute-start(bf16[1,32,4,1,128]{4,1,3,2,0:T(8,128)(2,1)} %get-tuple-element.53), channel_id=1, source_target_pairs={{0,1},{1,2},{2,3},{4,5},{5,6},{6,7},{8,9},{9,10},{10,11},{12,13},{... | collective-permute-start | bytes 98312 | tf_op jit(solution)/shard_map/ppermute | solution.py:19
  82.6 41.7 %copy-start.55 = (f32[1,4]{1,0:T(1,128)S(1)}, f32[1,4]{1,0:T(1,128)}, u32[]{:S(2)}) copy-start(f32[1,4]{1,0:T(1,128)} %param.12) | copy-start | bytes 52
  82.6 41.7 %copy-start.56 = (f32[4]{0:T(128)S(1)}, f32[4]{0:T(128)}, u32[]{:S(2)}) copy-start(f32[4]{0:T(128)} %param.18) | copy-start | bytes 52
  82.6 42.0 %copy-start.48 = (f32[64,4]{0,1:T(4,128)S(1)}, f32[64,4]{0,1:T(4,128)}, u32[]{:S(2)}) copy-start(f32[64,4]{0,1:T(4,128)} %param.21) | copy-start | bytes 3076
  149.7 14.2 %collective-permute-start.13 = (bf16[2,1,64,1,8,128]{5,2,4,3,1,0:T(8,128)(2,1)S(1)}, bf16[2,1,64,1,8,128]{5,2,4,3,1,0:T(8,128)(2,1)S(1)}, u32[]{:S(2)}, u32[]{:S(2)}) collective-permute-start(bf16[2,1,64,1,8,128]{5,2,4,3,1,0:T(8,128)(2,1)S(1)} %get-tuple-element.48), channel_id=1, source_target_pairs={{4,0},{8,4},{12,8},{5,1},{9,5},{13,9},{6,2},{10,6},{14,10},{7,3},{... | collective-permute-start | bytes 786440 | tf_op jit(solution)/shard_map/ppermute | solution.py:21
  151.0 12.9 %collective-permute-start.12 = (bf16[2,1,64,1,8,128]{5,2,4,3,1,0:T(8,128)(2,1)S(1)}, bf16[2,1,64,1,8,128]{5,2,4,3,1,0:T(8,128)(2,1)S(1)}, u32[]{:S(2)}, u32[]{:S(2)}) collective-permute-start(bf16[2,1,64,1,8,128]{5,2,4,3,1,0:T(8,128)(2,1)S(1)} %get-tuple-element.47), channel_id=1, source_target_pairs={{0,4},{4,8},{8,12},{1,5},{5,9},{9,13},{2,6},{6,10},{10,14},{3,7},{... | collective-permute-start | bytes 786440 | tf_op jit(solution)/shard_map/ppermute | solution.py:19
  162.9 128.3 %copy-start.14 = (f32[27,2048]{1,0:T(8,128)S(1)}, f32[27,2048]{1,0:T(8,128)}, u32[]{:S(2)}) copy-start(f32[27,2048]{1,0:T(8,128)} %param.20) | copy-start | bytes 663556
  163.9 129.1 %collective-permute-start.15 = (bf16[2,1,64,4,1,128]{5,2,4,3,1,0:T(8,128)(2,1)S(1)}, bf16[2,1,64,4,1,128]{5,2,4,3,1,0:T(8,128)(2,1)S(1)}, u32[]{:S(2)}, u32[]{:S(2)}) collective-permute-start(bf16[2,1,64,4,1,128]{5,2,4,3,1,0:T(8,128)(2,1)S(1)} %get-tuple-element.42), channel_id=1, source_target_pairs={{1,0},{2,1},{3,2},{5,4},{6,5},{7,6},{9,8},{10,9},{11,10},{13,12},{... | collective-permute-start | bytes 393224 | tf_op jit(solution)/shard_map/ppermute | solution.py:21
  165.2 127.8 %collective-permute-start.14 = (bf16[2,1,64,4,1,128]{5,2,4,3,1,0:T(8,128)(2,1)S(1)}, bf16[2,1,64,4,1,128]{5,2,4,3,1,0:T(8,128)(2,1)S(1)}, u32[]{:S(2)}, u32[]{:S(2)}) collective-permute-start(bf16[2,1,64,4,1,128]{5,2,4,3,1,0:T(8,128)(2,1)S(1)} %get-tuple-element.41), channel_id=1, source_target_pairs={{0,1},{1,2},{2,3},{4,5},{5,6},{6,7},{8,9},{9,10},{10,11},{12,13},{... | collective-permute-start | bytes 393224 | tf_op jit(solution)/shard_map/ppermute | solution.py:19
  314.0 43.8 %copy-start.32 = (f32[27,128]{1,0:T(8,128)S(1)}, f32[27,128]{1,0:T(8,128)}, u32[]{:S(2)}) copy-start(f32[27,128]{1,0:T(8,128)} %param.19) | copy-start | bytes 41476
  (57 other events, 231.5 us)
Sparse Core Ops, SparseCore 0:
  163.8 127.3 all-reduce.6
where the time goes:
time: 380 us; the launch traced here: 376 us
  waiting for transfers between devices  125 us (33%)
  blocking collectives  78.7 us (21%)
  matrix products  54.8 us (14%)
  starting transfers between devices  48.4 us (13%)
  local copies, waits for them, and re-layouts  35.4 us (9%)
  between operations  23.2 us (6%)
  other arithmetic  10.9 us (3%)
    psum x1, waiting for transfers between devices, per_device(): h1, h2, hd = lax.psum((h1, h2, hd), ('dp', 'gx', 'gy'))  122 us
    psum x1, blocking collectives, per_device(): h1, h2, hd = lax.psum((h1, h2, hd), ('dp', 'gx', 'gy'))  39.5 us
    psum x1, blocking collectives, per_device(): lax.psum((jnp.sum(act2, axis=(2, 3, 4)), jnp.sum(slope2 * t2, axis=(2, 3,...  39.3 us
    ppermute x8, starting transfers between devices, extended(): lax.ppermute(tail, axis, [(i, (i + 1) % count) for i in range(ends)])  38 us
    conv_general_dilated x8, matrix products, convolve(): lax.conv_general_dilated(pad_depth(padded), kernel, (1, 1, 1), 'VALID', d...  28.8 us
    dot_general x81, matrix products, correlate(): jnp.einsum('bixyz,boxyz->oi', window, grads, preferred_element_type=jnp.f...  25.3 us
    unnamed x145, local copies, waits for them, and re-layouts  13.8 us
    ppermute x8, starting transfers between devices, extended(): lax.ppermute(head, axis, [((i + 1) % count, i) for i in range(ends)])  10.3 us
  transfers between devices with their start and end apart: 17, of which 2 were waited for; matrix products, arithmetic and copies ran while one was open for 5% of the time, Pallas kernels for 0%

commit v1 on v0

--- a/solution.py
+++ b/solution.py
@@ -121,7 +121,7 @@
     tg1 = (bend1 * t1 * da1 + slope1 * tda1).astype(jnp.bfloat16)
     h1 = correlate(padded_in, tg1)
     h2 = correlate(pa1, tg2) + correlate(pta1, g2)
-    h1, h2, hd = lax.psum((h1, h2, hd), ("dp", "gx", "gy"))
+    h1, h2, hd = jax.lax.psum(jax.lax.psum((h1, h2, hd), axis_name=("gx", "gy")), axis_name="dp")
     field = tda1 * cells
     quad = jnp.sum(dir1 * h1) + jnp.sum(dir2 * h2) + jnp.sum(dir_head * hd)
     length = jnp.sum(dir1 * dir1) + jnp.sum(dir2 * dir2) + jnp.sum(dir_head * dir_head)

time: 380 us -> 401 us (1.055)
  blocking collectives: 78.7 us -> 118 us
  waiting for transfers between devices: 125 us -> 106 us
    psum x1 -> x2, blocking collectives: 39.5 us -> 78.6 us  [the longest x1 75.2 us: per_device(): jax.lax.psum((h1, h2, hd), axis_name=('gx', 'gy'))]
    psum x1 -> x2, waiting for transfers between devices: 122 us -> 103 us  [the longest x1 103 us: per_device(): jax.lax.psum((h1, h2, hd), axis_name=('gx', 'gy'))]
  transfers between devices with their start and end apart: 17 -> 18, of which waited for: 2 -> 2; matrix products, arithmetic and copies ran while one was open for 5% -> 11% of each run, Pallas kernels for 0% -> 0%
where the time goes in v1:
time: 401 us; the launch traced here: 397 us
  blocking collectives  118 us (29%)
  waiting for transfers between devices  106 us (26%)
  matrix products  54.8 us (14%)
  starting transfers between devices  48.4 us (12%)
  local copies, waits for them, and re-layouts  35.3 us (9%)
  between operations  23.1 us (6%)
  other arithmetic  11.4 us (3%)
    psum x1, waiting for transfers between devices, per_device(): jax.lax.psum((h1, h2, hd), axis_name=('gx', 'gy'))  103 us
    psum x1, blocking collectives, per_device(): jax.lax.psum((h1, h2, hd), axis_name=('gx', 'gy'))  75.2 us
    psum x1, blocking collectives, per_device(): lax.psum((jnp.sum(act2, axis=(2, 3, 4)), jnp.sum(slope2 * t2, axis=(2, 3,...  39.2 us
    ppermute x8, starting transfers between devices, extended(): lax.ppermute(tail, axis, [(i, (i + 1) % count) for i in range(ends)])  38 us
    conv_general_dilated x8, matrix products, convolve(): lax.conv_general_dilated(pad_depth(padded), kernel, (1, 1, 1), 'VALID', d...  28.8 us
    dot_general x81, matrix products, correlate(): jnp.einsum('bixyz,boxyz->oi', window, grads, preferred_element_type=jnp.f...  25.2 us
    unnamed x145, local copies, waits for them, and re-layouts  13.8 us
    ppermute x8, starting transfers between devices, extended(): lax.ppermute(head, axis, [((i + 1) % count, i) for i in range(ends)])  10.3 us
  transfers between devices with their start and end apart: 18, of which 2 were waited for; matrix products, arithmetic and copies ran while one was open for 11% of the time, Pallas kernels for 0%

profile of v1, /device:TPU:0, one launch (start us, length us, event | category | flops | bytes accessed | tf_op | source)
XLA Modules:
  0.0 397.2 jit_solution(15414566915685727354)
XLA Ops:
  8.0 4.9 %collective-permute-start = (bf16[1,4,1,8,128]{4,1,3,2,0:T(4,128)(2,1)S(1)}, bf16[1,4,1,8,128]{4,1,3,2,0:T(4,128)(2,1)S(1)}, u32[]{:S(2)}, u32[]{:S(2)}) collective-permute-start(bf16[1,4,1,8,128]{4,1,3,2,0:T(4,128)(2,1)S(1)} %get-tuple-element.62), channel_id=1, source_target_pairs={{0,4},{4,8},{8,12},{1,5},{5,9},{9,13},{2,6},{6,10},{10,14},{3,7},{... | collective-permute-start | bytes 24584 | tf_op jit(solution)/shard_map/ppermute | solution.py:19
  15.0 3.5 collective-permute-done.1
  19.8 4.5 %collective-permute-start.2 = (bf16[1,4,4,1,128]{4,1,3,2,0:T(4,128)(2,1)S(1)}, bf16[1,4,4,1,128]{4,1,3,2,0:T(4,128)(2,1)S(1)}, u32[]{:S(2)}, u32[]{:S(2)}) collective-permute-start(bf16[1,4,4,1,128]{4,1,3,2,0:T(4,128)(2,1)S(1)} %get-tuple-element.59), channel_id=1, source_target_pairs={{0,1},{1,2},{2,3},{4,5},{5,6},{6,7},{8,9},{9,10},{10,11},{12,13},{... | collective-permute-start | bytes 12296 | tf_op jit(solution)/shard_map/ppermute | solution.py:19
  24.3 2.0 reshape.567
  31.9 6.4 %fusion.38 = f32[2,8,8,17,32]{4,2,3,1,0:T(8,128)S(1)} fusion(bf16[3,3,3,32,4]{4,3,2,1,0:T(8,128)(2,1)S(1)} %reshape.565, f32[32]{0:T(128)S(1)} %copy-done.51, pred[8,17]{0,1:T(8,128)(4,1)S(1)} %copy-done.55, bf16[4,4,10,1,7,2]{4,0,5,2,1,3:T(4,128)(2,1)S(1)} %slice.473, bf16[4,4,10,1,8,17]{4,0,5,2,1,3:T(4,128)(2,1)S(1)} %copy.299), kind=kOutput, calls=%fused_computation.77 | convolution fusion | flops 15325696 | bytes 333704 | tf_op jit(solution)/shard_map/conv_general_dilated | solution.py:42
  38.3 7.7 %multiply_convert_fusion.1 = (bf16[2,8,8,17,32]{4,2,3,1,0:T(8,128)(2,1)S(1)}, bf16[2,8,8,17,32]{4,2,3,1,0:T(8,128)(2,1)S(1)}, f32[2,8,8,17,32]{4,2,3,1,0:T(8,128)}) fusion(f32[2,8,8,17,32]{4,2,3,1,0:T(8,128)S(1)} %fusion.38, bf16[3,3,3,32,4]{4,3,2,1,0:T(8,128)(2,1)S(1)} %reshape.566, bf16[4,4,10,1,7,2]{4,0,5,2,1,3:T(4,128)(2,1)S(1)} %slice.473, ...), kind=kOutput, calls=%fused_computation.95 | convolution fusion | flops 16022016 | bytes 890632 | tf_op jit(solution)/shard_map/conv_general_dilated | solution.py:42
  48.4 4.9 %collective-permute-start.4 = (bf16[1,32,1,8,128]{4,1,3,2,0:T(8,128)(2,1)S(1)}, bf16[1,32,1,8,128]{4,1,3,2,0:T(8,128)(2,1)S(1)}, u32[]{:S(2)}, u32[]{:S(2)}) collective-permute-start(bf16[1,32,1,8,128]{4,1,3,2,0:T(8,128)(2,1)S(1)} %bitcast.755), channel_id=1, source_target_pairs={{0,4},{4,8},{8,12},{1,5},{5,9},{9,13},{2,6},{6,10},{10,14},{3,7},{... | collective-permute-start | bytes 196616 | tf_op jit(solution)/shard_map/ppermute | solution.py:19
  55.6 5.4 %collective-permute-start.8 = (bf16[1,32,1,8,128]{4,1,3,2,0:T(8,128)(2,1)S(1)}, bf16[1,32,1,8,128]{4,1,3,2,0:T(8,128)(2,1)S(1)}, u32[]{:S(2)}, u32[]{:S(2)}) collective-permute-start(bf16[1,32,1,8,128]{4,1,3,2,0:T(8,128)(2,1)S(1)} %bitcast.756), channel_id=1, source_target_pairs={{0,4},{4,8},{8,12},{1,5},{5,9},{9,13},{2,6},{6,10},{10,14},{3,7},{... | collective-permute-start | bytes 196616 | tf_op jit(solution)/shard_map/ppermute | solution.py:19
  62.4 4.5 %collective-permute-start.6 = (bf16[1,32,4,1,128]{4,1,3,2,0:T(8,128)(2,1)S(1)}, bf16[1,32,4,1,128]{4,1,3,2,0:T(8,128)(2,1)S(1)}, u32[]{:S(2)}, u32[]{:S(2)}) collective-permute-start(bf16[1,32,4,1,128]{4,1,3,2,0:T(8,128)(2,1)S(1)} %get-tuple-element.57), channel_id=1, source_target_pairs={{0,1},{1,2},{2,3},{4,5},{5,6},{6,7},{8,9},{9,10},{10,11},{12,13},{... | collective-permute-start | bytes 98312 | tf_op jit(solution)/shard_map/ppermute | solution.py:19
  69.0 4.5 %collective-permute-start.10 = (bf16[1,32,4,1,128]{4,1,3,2,0:T(8,128)(2,1)}, bf16[1,32,4,1,128]{4,1,3,2,0:T(8,128)(2,1)S(1)}, u32[]{:S(2)}, u32[]{:S(2)}) collective-permute-start(bf16[1,32,4,1,128]{4,1,3,2,0:T(8,128)(2,1)} %get-tuple-element.55), channel_id=1, source_target_pairs={{0,1},{1,2},{2,3},{4,5},{5,6},{6,7},{8,9},{9,10},{10,11},{12,13},{... | collective-permute-start | bytes 98312 | tf_op jit(solution)/shard_map/ppermute | solution.py:19
  78.7 1.9 convolution_select_fusion.2
  80.7 1.9 fusion.37
  82.6 2.4 select_reduce_fusion
  85.1 39.2 %all-reduce.4 = (f32[1,64]{1,0:T(1,128)S(1)}, f32[1,64]{1,0:T(1,128)S(1)}) all-reduce(f32[1,64]{1,0:T(1,128)S(1)} %bitcast.760, f32[1,64]{1,0:T(1,128)S(1)} %bitcast.759), channel_id=1, replica_groups=mesh['dp'=2,'gx'=4,'gy'=4] {'gx','gy'}, use_global_device_ids=true, to_apply=%region_1.2 | all-reduce | flops 128 | bytes 1024 | tf_op jit(solution)/shard_map/psum | solution.py:97
  125.7 2.1 multiply_convert_fusion
  150.4 4.6 %collective-permute-start.12 = (bf16[2,1,64,1,8,128]{5,2,4,3,1,0:T(8,128)(2,1)S(1)}, bf16[2,1,64,1,8,128]{5,2,4,3,1,0:T(8,128)(2,1)S(1)}, u32[]{:S(2)}, u32[]{:S(2)}) collective-permute-start(bf16[2,1,64,1,8,128]{5,2,4,3,1,0:T(8,128)(2,1)S(1)} %get-tuple-element.49), channel_id=1, source_target_pairs={{0,4},{4,8},{8,12},{1,5},{5,9},{9,13},{2,6},{6,10},{10,14},{3,7},{... | collective-permute-start | bytes 786440 | tf_op jit(solution)/shard_map/ppermute | solution.py:19
  164.6 4.6 %collective-permute-start.14 = (bf16[2,1,64,4,1,128]{5,2,4,3,1,0:T(8,128)(2,1)S(1)}, bf16[2,1,64,4,1,128]{5,2,4,3,1,0:T(8,128)(2,1)S(1)}, u32[]{:S(2)}, u32[]{:S(2)}) collective-permute-start(bf16[2,1,64,4,1,128]{5,2,4,3,1,0:T(8,128)(2,1)S(1)} %get-tuple-element.43), channel_id=1, source_target_pairs={{0,1},{1,2},{2,3},{4,5},{5,6},{6,7},{8,9},{9,10},{10,11},{12,13},{... | collective-permute-start | bytes 393224 | tf_op jit(solution)/shard_map/ppermute | solution.py:19
  169.3 102.6 %all-reduce.9.cloned.1.call-done = f32[27,2048]{1,0:T(8,128)} async-done(((f32[27,2048]{1,0:T(8,128)}), f32[27,2048]{1,0:T(8,128)}) %all-reduce.9.cloned.1.call-update) | async-done | bytes 221200 | tf_op jit(solution)/shard_map/psum | solution.py:124
  275.6 3.3 convolution_select_fusion
  278.9 1.8 copy.592
  282.8 2.4 broadcast_multiply_fusion
  285.3 2.7 fusion.39
  298.7 75.2 %all-reduce.3 = (f32[27,128]{1,0:T(8,128)S(1)}, f32[64,4]{0,1:T(4,128)S(1)}) all-reduce(f32[27,128]{1,0:T(8,128)S(1)} %stack.291, f32[64,4]{0,1:T(4,128)S(1)} %add_multiply_fusion), channel_id=1, replica_groups=mesh['dp'=2,'gx'=4,'gy'=4] {'gx','gy'}, use_global_device_ids=true, to_apply=%region_4.5 | all-reduce | flops 3712 | bytes 29696 | tf_op jit(solution)/shard_map/psum | solution.py:124
  373.9 3.4 all-reduce.5
  (412 shorter events, 77.4 us)
Async XLA Ops:
  7.2 117.2 %copy-start = (f32[64,4]{0,1:T(4,128)S(1)}, f32[64,4]{0,1:T(4,128)}, u32[]{:S(2)}) copy-start(f32[64,4]{0,1:T(4,128)} %param.17) | copy-start | bytes 3076
  7.2 264.7 %all-reduce.9.cloned.1.call-start = ((), (), s32[]{:S(2)}) async-start(), calls=%async_computation | async-start | bytes 524288 | tf_op jit(solution)/shard_map/psum | solution.py:124
  8.0 6.2 %collective-permute-start = (bf16[1,4,1,8,128]{4,1,3,2,0:T(4,128)(2,1)S(1)}, bf16[1,4,1,8,128]{4,1,3,2,0:T(4,128)(2,1)S(1)}, u32[]{:S(2)}, u32[]{:S(2)}) collective-permute-start(bf16[1,4,1,8,128]{4,1,3,2,0:T(4,128)(2,1)S(1)} %get-tuple-element.62), channel_id=1, source_target_pairs={{0,4},{4,8},{8,12},{1,5},{5,9},{9,13},{2,6},{6,10},{10,14},{3,7},{... | collective-permute-start | bytes 24584 | tf_op jit(solution)/shard_map/ppermute | solution.py:19
  12.9 5.5 %collective-permute-start.1 = (bf16[1,4,1,8,128]{4,1,3,2,0:T(4,128)(2,1)S(1)}, bf16[1,4,1,8,128]{4,1,3,2,0:T(4,128)(2,1)S(1)}, u32[]{:S(2)}, u32[]{:S(2)}) collective-permute-start(bf16[1,4,1,8,128]{4,1,3,2,0:T(4,128)(2,1)S(1)} %get-tuple-element.61), channel_id=1, source_target_pairs={{4,0},{8,4},{12,8},{5,1},{9,5},{13,9},{6,2},{10,6},{14,10},{7,3},{... | collective-permute-start | bytes 24584 | tf_op jit(solution)/shard_map/ppermute | solution.py:21
  18.4 42.6 %copy-start.27 = (bf16[1,4,4,8,128]{4,1,3,2,0:T(4,128)(2,1)}, bf16[1,4,4,8,128]{4,1,3,2,0:T(4,128)(2,1)S(1)}, u32[]{:S(2)}) copy-start(bf16[1,4,4,8,128]{4,1,3,2,0:T(4,128)(2,1)S(1)} %constant_dynamic-update-slice_fusion) | copy-start | bytes 98308
  18.5 11.4 %collective-permute-start.3 = (bf16[1,4,4,1,128]{4,1,3,2,0:T(4,128)(2,1)S(1)}, bf16[1,4,4,1,128]{4,1,3,2,0:T(4,128)(2,1)S(1)}, u32[]{:S(2)}, u32[]{:S(2)}) collective-permute-start(bf16[1,4,4,1,128]{4,1,3,2,0:T(4,128)(2,1)S(1)} %get-tuple-element.60), channel_id=1, source_target_pairs={{1,0},{2,1},{3,2},{5,4},{6,5},{7,6},{9,8},{10,9},{11,10},{13,12},{... | collective-permute-start | bytes 12296 | tf_op jit(solution)/shard_map/ppermute | solution.py:21
  19.8 10.1 %collective-permute-start.2 = (bf16[1,4,4,1,128]{4,1,3,2,0:T(4,128)(2,1)S(1)}, bf16[1,4,4,1,128]{4,1,3,2,0:T(4,128)(2,1)S(1)}, u32[]{:S(2)}, u32[]{:S(2)}) collective-permute-start(bf16[1,4,4,1,128]{4,1,3,2,0:T(4,128)(2,1)S(1)} %get-tuple-element.59), channel_id=1, source_target_pairs={{0,1},{1,2},{2,3},{4,5},{5,6},{6,7},{8,9},{9,10},{10,11},{12,13},{... | collective-permute-start | bytes 12296 | tf_op jit(solution)/shard_map/ppermute | solution.py:19
  46.5 14.6 %collective-permute-start.5 = (bf16[1,32,1,8,128]{4,1,3,2,0:T(8,128)(2,1)S(1)}, bf16[1,32,1,8,128]{4,1,3,2,0:T(8,128)(2,1)S(1)}, u32[]{:S(2)}, u32[]{:S(2)}) collective-permute-start(bf16[1,32,1,8,128]{4,1,3,2,0:T(8,128)(2,1)S(1)} %bitcast.753), channel_id=1, source_target_pairs={{4,0},{8,4},{12,8},{5,1},{9,5},{13,9},{6,2},{10,6},{14,10},{7,3},{... | collective-permute-start | bytes 196616 | tf_op jit(solution)/shard_map/ppermute | solution.py:21
  48.4 12.7 %collective-permute-start.4 = (bf16[1,32,1,8,128]{4,1,3,2,0:T(8,128)(2,1)S(1)}, bf16[1,32,1,8,128]{4,1,3,2,0:T(8,128)(2,1)S(1)}, u32[]{:S(2)}, u32[]{:S(2)}) collective-permute-start(bf16[1,32,1,8,128]{4,1,3,2,0:T(8,128)(2,1)S(1)} %bitcast.755), channel_id=1, source_target_pairs={{0,4},{4,8},{8,12},{1,5},{5,9},{9,13},{2,6},{6,10},{10,14},{3,7},{... | collective-permute-start | bytes 196616 | tf_op jit(solution)/shard_map/ppermute | solution.py:19
  53.6 13.4 %collective-permute-start.9 = (bf16[1,32,1,8,128]{4,1,3,2,0:T(8,128)(2,1)S(1)}, bf16[1,32,1,8,128]{4,1,3,2,0:T(8,128)(2,1)S(1)}, u32[]{:S(2)}, u32[]{:S(2)}) collective-permute-start(bf16[1,32,1,8,128]{4,1,3,2,0:T(8,128)(2,1)S(1)} %bitcast.754), channel_id=1, source_target_pairs={{4,0},{8,4},{12,8},{5,1},{9,5},{13,9},{6,2},{10,6},{14,10},{7,3},{... | collective-permute-start | bytes 196616 | tf_op jit(solution)/shard_map/ppermute | solution.py:21
  55.6 11.5 %collective-permute-start.8 = (bf16[1,32,1,8,128]{4,1,3,2,0:T(8,128)(2,1)S(1)}, bf16[1,32,1,8,128]{4,1,3,2,0:T(8,128)(2,1)S(1)}, u32[]{:S(2)}, u32[]{:S(2)}) collective-permute-start(bf16[1,32,1,8,128]{4,1,3,2,0:T(8,128)(2,1)S(1)} %bitcast.756), channel_id=1, source_target_pairs={{0,4},{4,8},{8,12},{1,5},{5,9},{9,13},{2,6},{6,10},{10,14},{3,7},{... | collective-permute-start | bytes 196616 | tf_op jit(solution)/shard_map/ppermute | solution.py:19
  61.1 12.4 %collective-permute-start.7 = (bf16[1,32,4,1,128]{4,1,3,2,0:T(8,128)(2,1)S(1)}, bf16[1,32,4,1,128]{4,1,3,2,0:T(8,128)(2,1)S(1)}, u32[]{:S(2)}, u32[]{:S(2)}) collective-permute-start(bf16[1,32,4,1,128]{4,1,3,2,0:T(8,128)(2,1)S(1)} %get-tuple-element.58), channel_id=1, source_target_pairs={{1,0},{2,1},{3,2},{5,4},{6,5},{7,6},{9,8},{10,9},{11,10},{13,12},{... | collective-permute-start | bytes 98312 | tf_op jit(solution)/shard_map/ppermute | solution.py:21
  62.4 11.1 %collective-permute-start.6 = (bf16[1,32,4,1,128]{4,1,3,2,0:T(8,128)(2,1)S(1)}, bf16[1,32,4,1,128]{4,1,3,2,0:T(8,128)(2,1)S(1)}, u32[]{:S(2)}, u32[]{:S(2)}) collective-permute-start(bf16[1,32,4,1,128]{4,1,3,2,0:T(8,128)(2,1)S(1)} %get-tuple-element.57), channel_id=1, source_target_pairs={{0,1},{1,2},{2,3},{4,5},{5,6},{6,7},{8,9},{9,10},{10,11},{12,13},{... | collective-permute-start | bytes 98312 | tf_op jit(solution)/shard_map/ppermute | solution.py:19
  67.7 8.4 %collective-permute-start.11 = (bf16[1,32,4,1,128]{4,1,3,2,0:T(8,128)(2,1)}, bf16[1,32,4,1,128]{4,1,3,2,0:T(8,128)(2,1)S(1)}, u32[]{:S(2)}, u32[]{:S(2)}) collective-permute-start(bf16[1,32,4,1,128]{4,1,3,2,0:T(8,128)(2,1)} %get-tuple-element.56), channel_id=1, source_target_pairs={{1,0},{2,1},{3,2},{5,4},{6,5},{7,6},{9,8},{10,9},{11,10},{13,12},{... | collective-permute-start | bytes 98312 | tf_op jit(solution)/shard_map/ppermute | solution.py:21
  69.0 7.1 %collective-permute-start.10 = (bf16[1,32,4,1,128]{4,1,3,2,0:T(8,128)(2,1)}, bf16[1,32,4,1,128]{4,1,3,2,0:T(8,128)(2,1)S(1)}, u32[]{:S(2)}, u32[]{:S(2)}) collective-permute-start(bf16[1,32,4,1,128]{4,1,3,2,0:T(8,128)(2,1)} %get-tuple-element.55), channel_id=1, source_target_pairs={{0,1},{1,2},{2,3},{4,5},{5,6},{6,7},{8,9},{9,10},{10,11},{12,13},{... | collective-permute-start | bytes 98312 | tf_op jit(solution)/shard_map/ppermute | solution.py:19
  82.6 41.7 %copy-start.53 = (f32[1,4]{1,0:T(1,128)S(1)}, f32[1,4]{1,0:T(1,128)}, u32[]{:S(2)}) copy-start(f32[1,4]{1,0:T(1,128)} %param.12) | copy-start | bytes 52
  82.6 42.0 %copy-start.47 = (f32[64,4]{0,1:T(4,128)S(1)}, f32[64,4]{0,1:T(4,128)}, u32[]{:S(2)}) copy-start(f32[64,4]{0,1:T(4,128)} %param.21) | copy-start | bytes 3076
  149.1 14.1 %collective-permute-start.13 = (bf16[2,1,64,1,8,128]{5,2,4,3,1,0:T(8,128)(2,1)S(1)}, bf16[2,1,64,1,8,128]{5,2,4,3,1,0:T(8,128)(2,1)S(1)}, u32[]{:S(2)}, u32[]{:S(2)}) collective-permute-start(bf16[2,1,64,1,8,128]{5,2,4,3,1,0:T(8,128)(2,1)S(1)} %get-tuple-element.50), channel_id=1, source_target_pairs={{4,0},{8,4},{12,8},{5,1},{9,5},{13,9},{6,2},{10,6},{14,10},{7,3},{... | collective-permute-start | bytes 786440 | tf_op jit(solution)/shard_map/ppermute | solution.py:21
  150.4 12.8 %collective-permute-start.12 = (bf16[2,1,64,1,8,128]{5,2,4,3,1,0:T(8,128)(2,1)S(1)}, bf16[2,1,64,1,8,128]{5,2,4,3,1,0:T(8,128)(2,1)S(1)}, u32[]{:S(2)}, u32[]{:S(2)}) collective-permute-start(bf16[2,1,64,1,8,128]{5,2,4,3,1,0:T(8,128)(2,1)S(1)} %get-tuple-element.49), channel_id=1, source_target_pairs={{0,4},{4,8},{8,12},{1,5},{5,9},{9,13},{2,6},{6,10},{10,14},{3,7},{... | collective-permute-start | bytes 786440 | tf_op jit(solution)/shard_map/ppermute | solution.py:19
  163.2 215.5 %all-reduce.11.cloned.1.call-start = ((), (), s32[]{:S(2)}) async-start(), calls=%async_computation.1 | async-start | bytes 524288 | tf_op jit(solution)/shard_map/psum | solution.py:124
  163.3 108.6 %collective-permute-start.15 = (bf16[2,1,64,4,1,128]{5,2,4,3,1,0:T(8,128)(2,1)S(1)}, bf16[2,1,64,4,1,128]{5,2,4,3,1,0:T(8,128)(2,1)S(1)}, u32[]{:S(2)}, u32[]{:S(2)}) collective-permute-start(bf16[2,1,64,4,1,128]{5,2,4,3,1,0:T(8,128)(2,1)S(1)} %get-tuple-element.44), channel_id=1, source_target_pairs={{1,0},{2,1},{3,2},{5,4},{6,5},{7,6},{9,8},{10,9},{11,10},{13,12},{... | collective-permute-start | bytes 393224 | tf_op jit(solution)/shard_map/ppermute | solution.py:21
  164.6 107.3 %collective-permute-start.14 = (bf16[2,1,64,4,1,128]{5,2,4,3,1,0:T(8,128)(2,1)S(1)}, bf16[2,1,64,4,1,128]{5,2,4,3,1,0:T(8,128)(2,1)S(1)}, u32[]{:S(2)}, u32[]{:S(2)}) collective-permute-start(bf16[2,1,64,4,1,128]{5,2,4,3,1,0:T(8,128)(2,1)S(1)} %get-tuple-element.43), channel_id=1, source_target_pairs={{0,1},{1,2},{2,3},{4,5},{5,6},{6,7},{8,9},{9,10},{10,11},{12,13},{... | collective-permute-start | bytes 393224 | tf_op jit(solution)/shard_map/ppermute | solution.py:19
  297.5 80.5 %copy-start.31 = (f32[27,128]{1,0:T(8,128)S(1)}, f32[27,128]{1,0:T(8,128)}, u32[]{:S(2)}) copy-start(f32[27,128]{1,0:T(8,128)} %param.19) | copy-start | bytes 41476
  297.5 81.1 %copy-start.14 = (f32[27,2048]{1,0:T(8,128)S(1)}, f32[27,2048]{1,0:T(8,128)}, u32[]{:S(2)}) copy-start(f32[27,2048]{1,0:T(8,128)} %param.20) | copy-start | bytes 663556
  (58 other events, 281.3 us)
Sparse Core Ops, SparseCore 0:
  163.3 108.5 all-reduce.8
  274.2 17.2 all-reduce.10
